TPU v7x, 32 devices: a whole 2x2x4 slice. The times are simulated.
32 devices in a mesh: dp: 16 (over z, y, x), tm: 2 (over core).
Axes of the slice: x: 2, y: 2, z: 4, core: 2. Of those that a mesh axis runs over, the one named last changes fastest.
Arguments:
- hidden: bfloat16 [32, 256, 4096], P('dp', 'tm'), may hold values from -6 to 6
- first_weight: bfloat16 [4096, 1024], P('dp'), may hold values from -0.09375 to 0.09375
- first_bias: float32 [1024], replicated, may hold values from -3 to 3
- second_weight: float32 [1024], replicated, may hold values from -0.1875 to 0.1875
- second_bias: float32 [1], replicated, may hold values from -3 to 3
- rewards: float32 [32, 256], P('dp', 'tm'), may hold values from -0.8 to 0.8
- dones: int32 [32, 256], P('dp', 'tm'), may hold values 0 or 1
- lengths: int32 [32], P('dp'), may hold values from 128 to 256
- discount: float32 [32], P('dp'), may hold values from 0.96 to 1
- trace: float32 [32], P('dp'), may hold values from 0.99609375 to 1
Outputs:
- advantages: float32 [32, 256], P('dp', 'tm')
- returns: float32 [32, 256], P('dp', 'tm')
All inputs are finite; a program needn't handle non-finite values. No bound on the sum of `dones` on one device may be relied on, other than what follows from the above.
Results may differ from a plain program's by a relative error of at most 0.0003.
Values may be sent and summed in bfloat16 or wider, within the bound.
No kernel may reach another device: no remote copies, remote signals or barrier semaphores. Data moves between devices by JAX's collectives and lax.ppermute only.
A program may use at most 64 MiB of HBM per device.

v0:
```python
import jax
import jax.numpy as jnp
from jax import lax
from jax.sharding import PartitionSpec as P


def passed_along(block, axis, distance):
    devices = range(lax.axis_size(axis))
    route = [(i - distance, i) for i in devices if i - distance in devices]
    return lax.ppermute(block, axis, route)


def pair_combine(earlier, later):
    return (earlier[0] * later[0], later[1] + later[0] * earlier[1])


def local_suffix(decay, delta):
    return lax.associative_scan(pair_combine, (decay, delta), reverse=True, axis=1)


def on_device(
    hidden,
    first_weight,
    first_bias,
    second_weight,
    second_bias,
    rewards,
    dones,
    lengths,
    discount,
    trace,
):
    traj_local, step_local, feature_count = hidden.shape
    row_count = traj_local * step_local
    token_rows = hidden.reshape(row_count, feature_count)
    whole_weight = lax.all_gather(first_weight, "dp", axis=0, tiled=True)
    pre = jnp.dot(token_rows, whole_weight, preferred_element_type=jnp.float32)
    values = jnp.dot(jax.nn.silu(pre + first_bias), second_weight, precision=lax.Precision.HIGHEST)
    values = (values + second_bias[0]).reshape(traj_local, step_local)
    time_index = lax.axis_index("tm") * step_local + jnp.arange(step_local, dtype=jnp.int32)
    live = (time_index[None, :] < lengths[:, None]).astype(jnp.float32)
    live_next = ((time_index + 1)[None, :] < lengths[:, None]).astype(jnp.float32)
    keep = 1.0 - dones.astype(jnp.float32)
    following = passed_along(values[:, :1], "tm", -1)
    value_next = jnp.concatenate([values[:, 1:], following], axis=1)
    gamma = discount[:, None]
    delta = live * (rewards + gamma * keep * live_next * value_next - values)
    decay = gamma * trace[:, None] * keep * live_next
    product, offset_gain = local_suffix(decay, delta)
    head_product = product[:, 0]
    head_offset = offset_gain[:, 0]

    def pass_back(turn, incoming):
        return passed_along(head_offset + head_product * incoming, "tm", -1)

    incoming = lax.fori_loop(
        0, lax.axis_size("tm") - 1, pass_back, jnp.zeros((traj_local,), jnp.float32)
    )
    gain = offset_gain + product * incoming[:, None]
    returns = live * (gain + values)
    local_count = jnp.sum(live)
    local_total = jnp.sum(gain)
    total, squares, count = lax.psum((local_total, jnp.sum(gain * gain), local_count), ("dp", "tm"))
    mean = total / count
    spread = squares / count - mean * mean
    advantages = live * (gain - mean) / jnp.sqrt(spread + 1e-06)
    return (advantages, returns)


def solution(mesh):
    in_specs = (
        P("dp", "tm", None),
        P("dp", None),
        P(),
        P(),
        P(),
        P("dp", "tm"),
        P("dp", "tm"),
        P("dp"),
        P("dp"),
        P("dp"),
    )
    out_specs = (P("dp", "tm"), P("dp", "tm"))
    return jax.shard_map(
        on_device, mesh=mesh, in_specs=in_specs, out_specs=out_specs, check_vma=False
    )
```

profile of v0, /device:TPU:0, one launch (start us, length us, event | category | flops | bytes accessed | tf_op | source)
XLA Modules:
  0.0 198.4 jit_solution(3137803917827415653)
XLA Ops:
  7.2 0.7 all-gather.2.cloned.1.call-update
  8.6 0.7 mul.149
  9.2 116.6 %all-gather.2.cloned.1.call-done = bf16[4096,1024]{1,0:T(8,128)(2,1)} async-done(((bf16[256,1024]{1,0:T(8,128)(2,1)}), bf16[4096,1024]{1,0:T(8,128)(2,1)}) %all-gather.2.cloned.1.call-update) | async-done | bytes 8388624 | tf_op jit(solution)/shard_map/all_gather | solution.py:36
  125.9 5.8 %convolution_add_fusion = f32[256,1024]{1,0:T(8,128)S(1)} fusion(bf16[256,4096]{1,0:T(8,128)(2,1)S(1)} %bitcast.25, bf16[4096,1024]{1,0:T(8,128)(2,1)} %all-gather.2.cloned.1.call-done, f32[1024]{0:T(1024)} %param.12), kind=kOutput, calls=%fused_computation | convolution fusion | flops 2147745792 | bytes 11538432 | tf_op jit(solution)/shard_map/dot_general | solution.py:37
  131.6 1.1 fusion
  132.8 1.3 collective-permute-start
  134.1 1.8 collective-permute-done
  135.9 0.7 compare_select_fusion.3
  136.6 0.2 slice.241
  136.7 0.2 slice.245
  136.9 0.2 slice.243
  137.0 0.2 slice.249
  141.1 0.2 slice.237
  141.2 0.2 slice.239
  144.3 0.1 pad.113
  144.7 0.1 pad.112
  144.9 0.1 pad.98
  145.2 0.2 add_reduce_fusion
  145.5 1.3 collective-permute-start.1
  146.8 1.8 collective-permute-done.1
  148.5 0.6 compare_select_fusion
  149.2 0.7 fusion.13
  149.8 38.6 %all-reduce.28 = (f32[]{:T(128)}, f32[]{:T(128)}, f32[]{:T(128)}) all-reduce(f32[]{:T(128)} %get-tuple-element.11, f32[]{:T(128)} %get-tuple-element.23, f32[]{:T(128)} %get-tuple-element.10), channel_id=1, replica_groups=mesh['dp'=16,'tm'=2] {'dp','tm'}, use_global_device_ids=true, to_apply=%region_5.6 | all-reduce | flops 3 | bytes 24 | tf_op jit(solution)/shard_map/psum | solution.py:63
  190.9 0.6 fusion.11
  (114 shorter events, 7.3 us)
Async XLA Ops:
  7.2 118.7 %copy-start = (bf16[2,128,4096]{2,1,0:T(8,128)(2,1)S(1)}, bf16[2,128,4096]{2,1,0:T(8,128)(2,1)}, u32[]{:S(2)}) copy-start(bf16[2,128,4096]{2,1,0:T(8,128)(2,1)} %param.10) | copy-start | bytes 6291460
  7.2 118.6 %all-gather.2.cloned.1.call-start = ((), (), s32[]{:S(2)}) async-start(), calls=%async_computation | async-start | bytes 8912896 | tf_op jit(solution)/shard_map/all_gather | solution.py:36
  125.8 5.8 %copy-start.5 = (f32[1024]{0:T(1024)S(1)}, f32[1024]{0:T(1024)}, u32[]{:S(2)}) copy-start(f32[1024]{0:T(1024)} %param.13) | copy-start | bytes 12292
  125.8 10.0 %copy-start.1 = (s32[2]{0:T(128)S(1)}, s32[2]{0:T(128)}, u32[]{:S(2)}) copy-start(s32[2]{0:T(128)} %param.17) | copy-start | bytes 28
  125.8 10.0 %copy-start.2 = (s32[2,128]{1,0:T(2,128)S(1)}, s32[2,128]{1,0:T(2,128)}, u32[]{:S(2)}) copy-start(s32[2,128]{1,0:T(2,128)} %param.16) | copy-start | bytes 3076
  125.8 10.0 %copy-start.3 = (f32[2,128]{1,0:T(2,128)S(1)}, f32[2,128]{1,0:T(2,128)}, u32[]{:S(2)}) copy-start(f32[2,128]{1,0:T(2,128)} %param.15) | copy-start | bytes 3076
  125.8 10.0 %copy-start.4 = (f32[2]{0:T(128)S(1)}, f32[2]{0:T(128)}, u32[]{:S(2)}) copy-start(f32[2]{0:T(128)} %param.18) | copy-start | bytes 28
  132.8 3.1 %collective-permute-start = (f32[2,1]{1,0:T(2,128)S(1)}, f32[2,1]{1,0:T(2,128)S(1)}, u32[]{:S(2)}, u32[]{:S(2)}) collective-permute-start(f32[2,1]{1,0:T(2,128)S(1)} %bitcast.37), channel_id=1, source_target_pairs={{1,0},{3,2},{5,4},{7,6},{9,8},{11,10},{13,12},{15,14},{17,16},{19,... | collective-permute-start | bytes 32 | tf_op jit(solution)/shard_map/ppermute | solution.py:10
  145.5 3.0 %collective-permute-start.1 = (f32[2]{0:T(128)S(1)}, f32[2]{0:T(128)S(1)}, u32[]{:S(2)}, u32[]{:S(2)}) collective-permute-start(f32[2]{0:T(128)S(1)} %add_reduce_fusion), channel_id=1, source_target_pairs={{1,0},{3,2},{5,4},{7,6},{9,8},{11,10},{13,12},{15,14},{17,16},{19,... | collective-permute-start | bytes 32 | tf_op jit(solution)/shard_map/while/body/eval_jaxpr/ppermute | solution.py:10
Sparse Core Ops, SparseCore 0:
  10.8 115.0 all-gather.1
where the time goes:
time: 199 us; the launch traced here: 198 us
  waiting for transfers between devices  121 us (61%)
  blocking collectives  38.6 us (19%)
  between operations  17.4 us (9%)
  local copies, waits for them, and re-layouts  7.3 us (4%)
  matrix products  6.84 us (3%)
  other arithmetic  4.86 us (2%)
  starting transfers between devices  2.61 us (1%)
    all_gather x1, waiting for transfers between devices, on_device(): whole_weight = lax.all_gather(first_weight, 'dp', axis=0, tiled=True)  117 us
    psum x1, blocking collectives, on_device(): lax.psum((local_total, jnp.sum(gain * gain), local_count), ('dp', 'tm'))  38.6 us
    dot_general x1, matrix products, on_device(): pre = jnp.dot(token_rows, whole_weight, preferred_element_type=jnp.float32)  5.75 us
    slice x42, local copies, waits for them, and re-layouts, local_suffix(): lax.associative_scan(pair_combine, (decay, delta), reverse=True, axis=1)  4.58 us
  transfers between devices with their start and end apart: 3, of which 3 were waited for; matrix products, arithmetic and copies ran while one was open for 0% of the time, Pallas kernels for 0%

commit v1 on v0

v1 whole, which is shorter than its diff:
```python
import functools

import jax
import jax.numpy as jnp
from jax import lax
from jax.experimental import pallas as pl
from jax.experimental.pallas import tpu as pltpu
from jax.sharding import PartitionSpec as P


BOTH = ("dp", "tm")


def ring_places(count):
    order = [0] + list(range(1, count, 2)) + [r for r in range(count - 1, 0, -1) if r % 2 == 0]
    return order, {r: i for i, r in enumerate(order)}


def routes(dp_size, tm_size):
    order, place = ring_places(dp_size // 4)
    first, second, up, down = [], [], [], []
    for d in range(dp_size):
        plane, q = d // 4, d % 4
        above = order[(place[plane] + 1) % len(order)]
        below = order[(place[plane] - 1) % len(order)]
        for t in range(tm_size):
            here = d * tm_size + t
            a, b = (1, 2) if t % 2 == 0 else (2, 1)
            first.append((here, (d ^ a) * tm_size + t))
            second.append((here, (d ^ b) * tm_size + t))
            up.append((here, (above * 4 + q) * tm_size + t))
            down.append((here, (below * 4 + q) * tm_size + t))
    return first, second, up, down


def passed_along(block, axis, distance):
    devices = range(lax.axis_size(axis))
    route = [(i - distance, i) for i in devices if i - distance in devices]
    return lax.ppermute(block, axis, route)


def pair_combine(earlier, later):
    return (earlier[0] * later[0], later[1] + later[0] * earlier[1])


def moments(gain, live):
    count, total = jnp.sum(live), jnp.sum(gain)
    deviation = live * (gain - total / jnp.maximum(count, 1.0))
    return count, total, jnp.sum(deviation * deviation)


def normalized(every, gain, live):
    counts, totals, squares = every[:, 0:1], every[:, 1:2], every[:, 2:3]
    count = jnp.sum(counts)
    mean = jnp.sum(totals) / count
    shift = totals / jnp.maximum(counts, 1.0) - mean
    spread = jnp.sum(squares + counts * shift * shift) / count
    return live * (gain - mean) / jnp.sqrt(jnp.full(gain.shape, spread + 1e-06))


def core_parity():
    return lax.bitwise_and(lax.axis_index("tm"), 1)


def columns_of(kind, k, planes, shard):
    d, parity = lax.axis_index("dp"), core_parity()
    order, place = ring_places(planes)
    plane, q = lax.shift_right_logical(d, 2), lax.bitwise_and(d, 3)
    source = 0
    for r in range(planes):
        source = jnp.where(plane == r, order[(place[r] - k) % planes], source)
    turns = (0, 1 + parity) if kind == "near" else (2 - parity, 3)
    return [(source * 4 + lax.bitwise_xor(q, turn)) * shard for turn in turns]


def bring_kernel(rows_ref, bias_ref, out_weight_ref, own_ref, constants_ref, sems):
    units = constants_ref.shape[1]
    mine = pl.ds(pl.multiple_of(core_parity() * units, units), units)
    copies = [
        pltpu.make_async_copy(rows_ref, own_ref, sems.at[0]),
        pltpu.make_async_copy(bias_ref.at[:, mine], constants_ref.at[0:1, :], sems.at[1]),
        pltpu.make_async_copy(out_weight_ref.at[:, mine], constants_ref.at[1:2, :], sems.at[2]),
    ]
    for copy in copies:
        copy.start()
    for copy in copies:
        copy.wait()


def dot_kernel(groups, planes, first_call, own_ref, other_ref, *refs):
    pre_ref = refs[-1]
    count = sum(len(x[2]) for x in groups)
    total = None if first_call else refs[count][...]
    taken = 0
    for kind, k, parts in groups:
        shard = refs[taken].shape[0]
        columns = [pl.ds(pl.multiple_of(at, shard), shard) for at in columns_of(kind, k, planes, shard)]
        for part in parts:
            block = jnp.concatenate([own_ref[:, columns[part]], other_ref[:, columns[part]]], axis=0)
            more = jnp.dot(block, refs[taken][...], preferred_element_type=jnp.float32)
            total = more if total is None else total + more
            taken += 1
    pre_ref[...] = total


def value_kernel(groups, planes, own_ref, other_ref, *refs):
    count = sum(len(x[2]) for x in groups)
    constants_ref, part_ref, pre_ref = refs[count + 1 :]
    dot_kernel(groups, planes, False, own_ref, other_ref, *refs[: count + 1], pre_ref)
    rows, units = pre_ref.shape
    bias, out_weight = constants_ref[0:1, :], constants_ref[1:2, :]
    for side in range(2):
        for at in range(0, rows // 2, 128):
            v = pre_ref[side * (rows // 2) + at : side * (rows // 2) + at + 128, :] + bias
            weighted = v / (1.0 + jnp.exp(-v)) * out_weight
            folded = sum(weighted[:, u : u + 128] for u in range(0, units, 128))
            part_ref[side : side + 1, at : at + 128] = jnp.sum(folded.T, axis=0, keepdims=True)


def prepare_kernel(
    rewards_ref, other_rewards_ref, dones_ref, other_dones_ref, lengths_ref, discount_ref, trace_ref, out_bias_ref, ready_ref, own_live_ref
):
    traj, step = rewards_ref.shape
    parity = core_parity()
    early = parity == 0

    def in_time(own, other):
        return jnp.concatenate([jnp.where(early, own, other), jnp.where(early, other, own)], axis=1)

    row = lax.broadcasted_iota(jnp.int32, (traj, 2 * step), 0)
    lane = lax.broadcasted_iota(jnp.int32, (traj, 2 * step), 1)

    def column(ref):
        out = jnp.full((traj, 2 * step), ref[0])
        for i in range(1, traj):
            out = jnp.where(row == i, ref[i], out)
        return out

    keep = 1.0 - in_time(dones_ref[...], other_dones_ref[...]).astype(jnp.float32)
    length = column(lengths_ref)
    live = jnp.where(lane < length, 1.0, 0.0)
    coef = jnp.where(lane + 1 < length, column(discount_ref) * keep, 0.0)
    ready_ref[0] = in_time(rewards_ref[...], other_rewards_ref[...])
    ready_ref[1] = coef
    ready_ref[2] = coef * column(trace_ref)
    ready_ref[3] = live
    ready_ref[4] = jnp.full((traj, 2 * step), out_bias_ref[0])
    own_live_ref[...] = jnp.where(early, live[:, :step], live[:, step:])


def scan_kernel(part_ref, swapped_ref, ready_ref, returns_ref, gain_ref, stats_ref):
    traj, steps = returns_ref.shape
    step = steps // 2
    early = core_parity() == 0
    both = part_ref[...] + pltpu.roll(swapped_ref[...], 1, 0)
    first, second = jnp.where(early, both[0:1], both[1:2]), jnp.where(early, both[1:2], both[0:1])
    values = jnp.concatenate(
        [
            jnp.concatenate([x[:, i * step : (i + 1) * step] for i in range(traj)], axis=0) for x in (first, second)
        ],
        axis=1,
    )
    values = values + ready_ref[4]
    lane = lax.broadcasted_iota(jnp.int32, values.shape, 1)
    decay, live = ready_ref[2], ready_ref[3]
    following = pltpu.roll(values, steps - 1, 1)
    gain = live * (ready_ref[0] + ready_ref[1] * jnp.where(lane == steps - 1, 0.0, following) - values)
    span = 1
    while span < steps:
        inside = lane < steps - span
        gain = gain + decay * jnp.where(inside, pltpu.roll(gain, steps - span, 1), 0.0)
        if 2 * span < steps:
            decay = decay * jnp.where(inside, pltpu.roll(decay, steps - span, 1), 0.0)
        span *= 2
    count, total, squares = moments(gain, live)
    slot = lax.broadcasted_iota(jnp.int32, stats_ref.shape, 2)
    stats_ref[...] = jnp.where(slot == 0, count, jnp.where(slot == 1, total, squares))
    gain_ref[...] = gain
    returns_ref[...] = live * (gain + values)


def final_kernel(every_ref, gain_ref, live_ref, advantages_ref):
    step = advantages_ref.shape[1]
    gain = jnp.where(core_parity() == 0, gain_ref[:, :step], gain_ref[:, step:])
    advantages_ref[...] = normalized(every_ref[...], gain, live_ref[...])


PARAMS = pltpu.CompilerParams(vmem_limit_bytes=8 * 2**20)
VMEM = pl.BlockSpec(memory_space=pltpu.VMEM)
SMEM = pl.BlockSpec(memory_space=pltpu.SMEM)


def kept(x):
    return pltpu.with_memory_space_constraint(x, pltpu.VMEM)


def values_in_kernels(planes, calls, own_rows, other_rows, first_bias, second_weight):
    rows, half = own_rows.shape[0], first_bias.shape[0] // 2
    row_vectors = [x.reshape(1, 2 * half) for x in (first_bias, second_weight)]
    acc = pltpu.VMEM((2 * rows, half), jnp.float32)
    other_rows = kept(other_rows)
    own_rows, constants = pl.pallas_call(
        bring_kernel,
        out_shape=(pltpu.VMEM(own_rows.shape, own_rows.dtype), pltpu.VMEM((2, half), jnp.float32)),
        in_specs=[pl.BlockSpec(memory_space=pl.ANY)] * 3,
        out_specs=(VMEM,) * 2,
        scratch_shapes=[pltpu.SemaphoreType.DMA((3,))],
        compiler_params=PARAMS,
    )(own_rows, *row_vectors)
    own_rows, constants, pre = kept(own_rows), kept(constants), []
    for at, call in enumerate(calls):
        groups = [(kind, k, tuple(sorted(blocks))) for kind, k, blocks in call]
        weights = [kept(blocks[i]) for _, _, blocks in call for i in sorted(blocks)]
        if at + 1 < len(calls):
            pre = [
                pl.pallas_call(
                    functools.partial(dot_kernel, groups, planes, not pre),
                    out_shape=acc,
                    in_specs=[VMEM] * (2 + len(weights) + len(pre)),
                    out_specs=VMEM,
                    input_output_aliases={2 + len(weights): 0} if pre else {},
                    compiler_params=PARAMS,
                )(own_rows, other_rows, *weights, *pre)
            ]
        else:
            part = pl.pallas_call(
                functools.partial(value_kernel, groups, planes),
                out_shape=pltpu.VMEM((2, rows), jnp.float32),
                in_specs=[VMEM] * (4 + len(weights)),
                out_specs=VMEM,
                scratch_shapes=[acc],
                compiler_params=PARAMS,
            )(own_rows, other_rows, *weights, *pre, constants)
    return part


def on_device(hidden, first_weight, first_bias, second_weight, second_bias, rewards, dones, lengths, discount, trace):
    dp_size, tm_size = lax.axis_size("dp"), lax.axis_size("tm")
    traj, step, feature_count = hidden.shape
    shard, unit_count = first_weight.shape
    half = unit_count // 2
    rows = traj * step
    devices = dp_size * tm_size
    planes = dp_size // 4
    order, place = ring_places(planes)
    first, second, up, down = routes(dp_size, tm_size)
    pair = [(i, i ^ 1) for i in range(tm_size)]
    parity = core_parity()

    own = lax.dynamic_slice(first_weight, (0, parity * half), (shard, half))
    other_hidden = lax.ppermute(hidden, "tm", pair)

    def sent(block, route):
        return lax.ppermute(block, BOTH, route)

    half_way = planes // 2
    near, far = {}, {}
    for way, route, turns in (("up", up, range(half_way + 1)), ("down", down, range(planes - 1, half_way, -1))):
        piece = own
        for k in turns:
            if k:
                piece = sent(piece, route)
            if k < 2 or way == "down":
                beside = sent(piece, first)
            else:
                beside = sent(beside, route)
            near[k] = (piece, beside)
            far[k] = (sent(piece, second), sent(beside, second))
    sequence = [0, 1] + list(range(planes - 1, half_way, -1)) + list(range(2, half_way + 1))
    calls, last = [[("near", 0, dict(enumerate(near[0])))]], 0
    for k in sequence[1:]:
        calls.append([("near", k, dict(enumerate(near[k]))), ("far", last, dict(enumerate(far[last])))])
        last = k
    calls.append([("far", last, dict(enumerate(far[last])))])

    other_rewards = lax.ppermute(rewards, "tm", pair)
    other_dones = lax.ppermute(dones, "tm", pair)

    own_rows, other_rows = hidden.reshape(rows, feature_count), other_hidden.reshape(rows, feature_count)
    if shard % 128 == 0 and rows % 128 == 0:
        part = values_in_kernels(planes, calls, own_rows, other_rows, first_bias, second_weight)
    else:
        pre = jnp.zeros((2 * rows, half), jnp.float32)
        for kind, k, blocks in sum(calls, []):
            for i, at in enumerate(columns_of(kind, k, planes, shard)):
                columns = [lax.dynamic_slice(x, (0, at), (rows, shard)) for x in (own_rows, other_rows)]
                pre = pre + jnp.dot(jnp.concatenate(columns), blocks[i], preferred_element_type=jnp.float32)
        bias, out_weight = (lax.dynamic_slice(x, (parity * half,), (half,)) for x in (first_bias, second_weight))
        part = jnp.sum(jax.nn.silu(pre + bias) * out_weight, axis=1).reshape(2, rows)
    swapped = lax.ppermute(part, "tm", pair)
    block = jax.ShapeDtypeStruct((traj, step), jnp.float32)
    pair_block = jax.ShapeDtypeStruct((traj, 2 * step), jnp.float32)
    if tm_size == 2:
        ready, own_live = pl.pallas_call(
            prepare_kernel,
            out_shape=(pltpu.VMEM((5, *pair_block.shape), jnp.float32), pltpu.VMEM(block.shape, jnp.float32)),
            in_specs=[VMEM] * 4 + [SMEM] * 4,
            out_specs=(VMEM,) * 2,
            compiler_params=PARAMS,
        )(rewards, other_rewards, dones, other_dones, lengths, discount, trace, second_bias)
        returns, gain, stats = pl.pallas_call(
            scan_kernel,
            out_shape=(
                pltpu.VMEM(pair_block.shape, jnp.float32),
                pltpu.VMEM(pair_block.shape, jnp.float32),
                pltpu.VMEM((devices, 1, 128), jnp.float32),
            ),
            in_specs=[VMEM] * 3,
            out_specs=(VMEM,) * 3,
            compiler_params=PARAMS,
        )(kept(part), kept(swapped), kept(ready))
    else:

        def in_time(own, other):
            early = parity == 0
            return jnp.concatenate([jnp.where(early, own, other), jnp.where(early, other, own)], axis=1)

        values = (part + swapped[::-1] + second_bias[0]).reshape(2, traj, step)
        values = in_time(values[0], values[1])
        time_index = (lax.axis_index("tm") - parity) * step + jnp.arange(2 * step, dtype=jnp.int32)
        live = (time_index[None, :] < lengths[:, None]).astype(jnp.float32)
        live_next = ((time_index + 1)[None, :] < lengths[:, None]).astype(jnp.float32)
        coef = discount[:, None] * (1.0 - in_time(dones, other_dones).astype(jnp.float32)) * live_next
        following = jnp.concatenate([values[:, 1:], passed_along(values[:, :1], "tm", -2)], axis=1)
        delta = live * (in_time(rewards, other_rewards) + coef * following - values)
        decay = coef * trace[:, None]
        product_to_end, offset = lax.associative_scan(pair_combine, (decay, delta), reverse=True, axis=1)
        incoming = jnp.zeros((traj,), jnp.float32)
        for _ in range(tm_size // 2 - 1):
            incoming = passed_along(offset[:, 0] + product_to_end[:, 0] * incoming, "tm", -2)
        gain = offset + product_to_end * incoming[:, None]
        slot = jnp.arange(128)
        count, total, squares = moments(gain, live)
        stats = jnp.where(slot == 0, count, jnp.where(slot == 1, total, squares))
        stats = jnp.broadcast_to(stats, (devices, 1, 128))
        returns = live * (gain + values)
    every = lax.all_to_all(stats, BOTH, 0, 0, tiled=True).reshape(devices, 128)
    returns = lax.dynamic_slice(returns, (0, parity * step), (traj, step))
    if tm_size == 2:
        advantages = pl.pallas_call(
            final_kernel, out_shape=block, in_specs=[VMEM] * 3, out_specs=VMEM, compiler_params=PARAMS
        )(every, kept(gain), kept(own_live))
    else:
        gain, live = (lax.dynamic_slice(x, (0, parity * step), (traj, step)) for x in (gain, live))
        advantages = normalized(every, gain, live)
    return (advantages, returns)


def solution(mesh):
    in_specs = (
        P("dp", "tm", None),
        P("dp", None),
        P(),
        P(),
        P(),
        P("dp", "tm"),
        P("dp", "tm"),
        P("dp"),
        P("dp"),
        P("dp"),
    )
    out_specs = (P("dp", "tm"), P("dp", "tm"))


    return jax.shard_map(on_device, mesh=mesh, in_specs=in_specs, out_specs=out_specs, check_vma=False)
```

time: 199 us -> 64.7 us (0.33)
  waiting for transfers between devices: 121 us -> 19.9 us
  blocking collectives: 38.6 us -> 0 us
  starting transfers between devices: 2.61 us -> 32.3 us
  between operations: 17.4 us -> 1.42 us
  matrix products: 6.84 us -> 0 us
  Pallas kernels: 0 us -> 6.66 us
  other arithmetic: 4.86 us -> 0 us
  local copies, waits for them, and re-layouts: 7.3 us -> 4.06 us
    all_gather x1 -> x0, waiting for transfers between devices: 117 us -> none  [on_device(): whole_weight = lax.all_gather(first_weight, 'dp', axis=0, tiled=True)]
    psum x1 -> x0, blocking collectives: 38.6 us -> none  [on_device(): lax.psum((local_total, jnp.sum(gain * gain), local_count), ('dp', 'tm'))]
    ppermute x2 -> x19, starting transfers between devices: 2.58 us -> 27.4 us  [the longest x15 26.2 us: sent(): return lax.ppermute(block, BOTH, route)]
    ppermute x2 -> x19, waiting for transfers between devices: 3.51 us -> 13.3 us  [the longest x15 12.9 us: sent(): return lax.ppermute(block, BOTH, route)]
    dot_general x2 -> x0, matrix products: 6.84 us -> none  [the longest x1 5.75 us: on_device(): pre = jnp.dot(token_rows, whole_weight, preferred_element_type=jnp.float32)]
    pallas_call x0 -> x9, Pallas kernels: none -> 6.66 us  [the longest x4 2.6 us: values_in_kernels(): pl.pallas_call(functools.partial(dot_kernel, groups, planes, not pre), ou...]
    all_to_all x0 -> x1, waiting for transfers between devices: none -> 6.61 us  [on_device(): every = lax.all_to_all(stats, BOTH, 0, 0, tiled=True).reshape(devices, 128)]
    all_to_all x0 -> x1, starting transfers between devices: none -> 4.97 us  [on_device(): every = lax.all_to_all(stats, BOTH, 0, 0, tiled=True).reshape(devices, 128)]
  transfers between devices with their start and end apart: 3 -> 20, of which waited for: 3 -> 9; matrix products, arithmetic and copies ran while one was open for 0% -> 1% of each run, Pallas kernels for 0% -> 5%
where the time goes in v1:
time: 64.7 us; the launch traced here: 64.4 us
  starting transfers between devices  32.3 us (50%)
  waiting for transfers between devices  19.9 us (31%)
  Pallas kernels  6.66 us (10%)
  local copies, waits for them, and re-layouts  4.06 us (6%)
  between operations  1.42 us (2%)
    ppermute x15, starting transfers between devices, sent(): return lax.ppermute(block, BOTH, route)  26.2 us
    ppermute x15, waiting for transfers between devices, sent(): return lax.ppermute(block, BOTH, route)  12.9 us
    all_to_all x1, waiting for transfers between devices, on_device(): every = lax.all_to_all(stats, BOTH, 0, 0, tiled=True).reshape(devices, 128)  6.61 us
    all_to_all x1, starting transfers between devices, on_device(): every = lax.all_to_all(stats, BOTH, 0, 0, tiled=True).reshape(devices, 128)  4.97 us
    unnamed x18, local copies, waits for them, and re-layouts  3.47 us
    pallas_call x4, Pallas kernels, values_in_kernels(): pl.pallas_call(functools.partial(dot_kernel, groups, planes, not pre), ou...  2.6 us
    pallas_call x1, Pallas kernels, on_device(): pl.pallas_call(scan_kernel, out_shape=(pltpu.VMEM(pair_block.shape, jnp.f...  1.48 us
  transfers between devices with their start and end apart: 20, of which 9 were waited for; matrix products, arithmetic and copies ran while one was open for 1% of the time, Pallas kernels for 5%

profile of v1, /device:TPU:0, one launch (start us, length us, event | category | flops | bytes accessed | tf_op | source)
XLA Modules:
  0.0 64.4 jit_solution(7268221532422209312)
XLA Ops:
  1.7 3.1 %collective-permute-start.1 = (bf16[256,512]{1,0:T(8,128)(2,1)S(1)}, bf16[256,512]{1,0:T(8,128)(2,1)S(1)}, u32[]{:S(2)}, u32[]{:S(2)}) collective-permute-start(bf16[256,512]{1,0:T(8,128)(2,1)S(1)} %constant_dynamic-slice_fusion.1.refs_0_), channel_id=1, source_target_pairs={{0,8},{1,9},{2,10},{3,11},{4,12},{5,13},{6,14},{7,15},{8,24},{9,25... | collective-permute-start | bytes 786440 | tf_op jit(solution)/shard_map/ppermute | solution.py:254
  4.8 1.5 %collective-permute-start.14 = (bf16[256,512]{1,0:T(8,128)(2,1)S(1)}, bf16[256,512]{1,0:T(8,128)(2,1)S(1)}, u32[]{:S(2)}, u32[]{:S(2)}) collective-permute-start(bf16[256,512]{1,0:T(8,128)(2,1)S(1)} %constant_dynamic-slice_fusion.1.refs_0_), channel_id=1, source_target_pairs={{0,2},{1,5},{2,0},{3,7},{4,6},{5,1},{6,4},{7,3},{8,10},{9,13},{10,... | collective-permute-start | bytes 786440 | tf_op jit(solution)/shard_map/ppermute | solution.py:254
  6.3 1.5 %collective-permute-start.13 = (bf16[256,512]{1,0:T(8,128)(2,1)S(1)}, bf16[256,512]{1,0:T(8,128)(2,1)S(1)}, u32[]{:S(2)}, u32[]{:S(2)}) collective-permute-start(bf16[256,512]{1,0:T(8,128)(2,1)S(1)} %constant_dynamic-slice_fusion.1.refs_0_), channel_id=1, source_target_pairs={{0,4},{1,3},{2,6},{3,1},{4,0},{5,7},{6,2},{7,5},{8,12},{9,11},{10,... | collective-permute-start | bytes 786440 | tf_op jit(solution)/shard_map/ppermute | solution.py:254
  7.8 1.3 %collective-permute-start.7 = (bf16[256,512]{1,0:T(8,128)(2,1)S(1)}, bf16[256,512]{1,0:T(8,128)(2,1)S(1)}, u32[]{:S(2)}, u32[]{:S(2)}) collective-permute-start(bf16[256,512]{1,0:T(8,128)(2,1)S(1)} %constant_dynamic-slice_fusion.1.refs_0_), channel_id=1, source_target_pairs={{0,16},{1,17},{2,18},{3,19},{4,20},{5,21},{6,22},{7,23},{8,0},{9,1... | collective-permute-start | bytes 786440 | tf_op jit(solution)/shard_map/ppermute | solution.py:254
  9.2 3.1 %collective-permute-done.1.refs_0_ = bf16[256,512]{1,0:T(8,128)(2,1)S(1)} collective-permute-done((bf16[256,512]{1,0:T(8,128)(2,1)S(1)}, bf16[256,512]{1,0:T(8,128)(2,1)S(1)}, u32[]{:S(2)}, u32[]{:S(2)}) %collective-permute-start.1) | collective-permute-done | bytes 262176 | tf_op jit(solution)/shard_map/ppermute | solution.py:254
  12.2 1.5 %collective-permute-start.4 = (bf16[256,512]{1,0:T(8,128)(2,1)S(1)}, bf16[256,512]{1,0:T(8,128)(2,1)S(1)}, u32[]{:S(2)}, u32[]{:S(2)}) collective-permute-start(bf16[256,512]{1,0:T(8,128)(2,1)S(1)} %collective-permute-done.1.refs_0_), channel_id=1, source_target_pairs={{0,2},{1,5},{2,0},{3,7},{4,6},{5,1},{6,4},{7,3},{8,10},{9,13},{10,... | collective-permute-start | bytes 786440 | tf_op jit(solution)/shard_map/ppermute | solution.py:254
  13.8 1.5 %collective-permute-start.15 = (bf16[256,512]{1,0:T(8,128)(2,1)S(1)}, bf16[256,512]{1,0:T(8,128)(2,1)S(1)}, u32[]{:S(2)}, u32[]{:S(2)}) collective-permute-start(bf16[256,512]{1,0:T(8,128)(2,1)S(1)} %collective-permute-done.14.refs_1_), channel_id=1, source_target_pairs={{0,4},{1,3},{2,6},{3,1},{4,0},{5,7},{6,2},{7,5},{8,12},{9,11},{10,... | collective-permute-start | bytes 786440 | tf_op jit(solution)/shard_map/ppermute | solution.py:254
  15.8 1.9 %collective-permute-done.7.refs_0_ = bf16[256,512]{1,0:T(8,128)(2,1)S(1)} collective-permute-done((bf16[256,512]{1,0:T(8,128)(2,1)S(1)}, bf16[256,512]{1,0:T(8,128)(2,1)S(1)}, u32[]{:S(2)}, u32[]{:S(2)}) %collective-permute-start.7) | collective-permute-done | bytes 262176 | tf_op jit(solution)/shard_map/ppermute | solution.py:254
  17.7 1.5 %collective-permute-start.9 = (bf16[256,512]{1,0:T(8,128)(2,1)S(1)}, bf16[256,512]{1,0:T(8,128)(2,1)S(1)}, u32[]{:S(2)}, u32[]{:S(2)}) collective-permute-start(bf16[256,512]{1,0:T(8,128)(2,1)S(1)} %collective-permute-done.7.refs_0_), channel_id=1, source_target_pairs={{0,2},{1,5},{2,0},{3,7},{4,6},{5,1},{6,4},{7,3},{8,10},{9,13},{10,... | collective-permute-start | bytes 786440 | tf_op jit(solution)/shard_map/ppermute | solution.py:254
  19.3 2.1 %collective-permute-done.4.refs_1_ = bf16[256,512]{1,0:T(8,128)(2,1)S(1)} collective-permute-done((bf16[256,512]{1,0:T(8,128)(2,1)S(1)}, bf16[256,512]{1,0:T(8,128)(2,1)S(1)}, u32[]{:S(2)}, u32[]{:S(2)}) %collective-permute-start.4) | collective-permute-done | bytes 262176 | tf_op jit(solution)/shard_map/ppermute | solution.py:254
  21.4 3.6 %collective-permute-start.2 = (bf16[256,512]{1,0:T(8,128)(2,1)S(1)}, bf16[256,512]{1,0:T(8,128)(2,1)S(1)}, u32[]{:S(2)}, u32[]{:S(2)}) collective-permute-start(bf16[256,512]{1,0:T(8,128)(2,1)S(1)} %collective-permute-done.1.refs_0_), channel_id=1, source_target_pairs={{0,8},{1,9},{2,10},{3,11},{4,12},{5,13},{6,14},{7,15},{8,24},{9,25... | collective-permute-start | bytes 786440 | tf_op jit(solution)/shard_map/ppermute | solution.py:254
  25.0 3.8 %collective-permute-start.5 = (bf16[256,512]{1,0:T(8,128)(2,1)S(1)}, bf16[256,512]{1,0:T(8,128)(2,1)S(1)}, u32[]{:S(2)}, u32[]{:S(2)}) collective-permute-start(bf16[256,512]{1,0:T(8,128)(2,1)S(1)} %collective-permute-done.4.refs_1_), channel_id=1, source_target_pairs={{0,8},{1,9},{2,10},{3,11},{4,12},{5,13},{6,14},{7,15},{8,24},{9,25... | collective-permute-start | bytes 786440 | tf_op jit(solution)/shard_map/ppermute | solution.py:254
  28.8 2.2 %collective-permute-start.8 = (bf16[256,512]{1,0:T(8,128)(2,1)S(1)}, bf16[256,512]{1,0:T(8,128)(2,1)S(1)}, u32[]{:S(2)}, u32[]{:S(2)}) collective-permute-start(bf16[256,512]{1,0:T(8,128)(2,1)S(1)} %collective-permute-done.7.refs_0_), channel_id=1, source_target_pairs={{0,4},{1,3},{2,6},{3,1},{4,0},{5,7},{6,2},{7,5},{8,12},{9,11},{10,... | collective-permute-start | bytes 786440 | tf_op jit(solution)/shard_map/ppermute | solution.py:254
  31.0 2.0 %collective-permute-start.10 = (bf16[256,512]{1,0:T(8,128)(2,1)S(1)}, bf16[256,512]{1,0:T(8,128)(2,1)S(1)}, u32[]{:S(2)}, u32[]{:S(2)}) collective-permute-start(bf16[256,512]{1,0:T(8,128)(2,1)S(1)} %collective-permute-done.9.refs_1_), channel_id=1, source_target_pairs={{0,4},{1,3},{2,6},{3,1},{4,0},{5,7},{6,2},{7,5},{8,12},{9,11},{10,... | collective-permute-start | bytes 786440 | tf_op jit(solution)/shard_map/ppermute | solution.py:254
  33.0 0.8 %collective-permute-done.5.refs_1_ = bf16[256,512]{1,0:T(8,128)(2,1)S(1)} collective-permute-done((bf16[256,512]{1,0:T(8,128)(2,1)S(1)}, bf16[256,512]{1,0:T(8,128)(2,1)S(1)}, u32[]{:S(2)}, u32[]{:S(2)}) %collective-permute-start.5) | collective-permute-done | bytes 262176 | tf_op jit(solution)/shard_map/ppermute | solution.py:254
  33.8 1.0 %collective-permute-start.3 = (bf16[256,512]{1,0:T(8,128)(2,1)S(1)}, bf16[256,512]{1,0:T(8,128)(2,1)S(1)}, u32[]{:S(2)}, u32[]{:S(2)}) collective-permute-start(bf16[256,512]{1,0:T(8,128)(2,1)S(1)} %collective-permute-done.2.refs_0_), channel_id=1, source_target_pairs={{0,4},{1,3},{2,6},{3,1},{4,0},{5,7},{6,2},{7,5},{8,12},{9,11},{10,... | collective-permute-start | bytes 786440 | tf_op jit(solution)/shard_map/ppermute | solution.py:254
  34.8 1.0 %collective-permute-start.6 = (bf16[256,512]{1,0:T(8,128)(2,1)S(1)}, bf16[256,512]{1,0:T(8,128)(2,1)S(1)}, u32[]{:S(2)}, u32[]{:S(2)}) collective-permute-start(bf16[256,512]{1,0:T(8,128)(2,1)S(1)} %collective-permute-done.5.refs_1_), channel_id=1, source_target_pairs={{0,4},{1,3},{2,6},{3,1},{4,0},{5,7},{6,2},{7,5},{8,12},{9,11},{10,... | collective-permute-start | bytes 786440 | tf_op jit(solution)/shard_map/ppermute | solution.py:254
  35.8 1.6 %copy-done.1 = bf16[2,128,4096]{2,1,0:T(8,128)(2,1)S(1)} copy-done((bf16[2,128,4096]{2,1,0:T(8,128)(2,1)S(1)}, bf16[2,128,4096]{2,1,0:T(8,128)(2,1)}, u32[]{:S(2)}) %copy-start.1) | copy-done | bytes 2097176
  41.6 2.1 %collective-permute-done.3.refs_0_ = bf16[256,512]{1,0:T(8,128)(2,1)S(1)} collective-permute-done((bf16[256,512]{1,0:T(8,128)(2,1)S(1)}, bf16[256,512]{1,0:T(8,128)(2,1)S(1)}, u32[]{:S(2)}, u32[]{:S(2)}) %collective-permute-start.3) | collective-permute-done | bytes 262176 | tf_op jit(solution)/shard_map/ppermute | solution.py:254
  43.7 2.8 %collective-permute-done.6.refs_1_ = bf16[256,512]{1,0:T(8,128)(2,1)S(1)} collective-permute-done((bf16[256,512]{1,0:T(8,128)(2,1)S(1)}, bf16[256,512]{1,0:T(8,128)(2,1)S(1)}, u32[]{:S(2)}, u32[]{:S(2)}) %collective-permute-start.6) | collective-permute-done | bytes 262176 | tf_op jit(solution)/shard_map/ppermute | solution.py:254
  49.6 1.5 %shard_map.120 = (f32[2,256]{1,0:T(2,128)S(1)}, f32[2,256]{1,0:T(2,128)S(1)}, f32[32,1,128]{2,1,0:T(1,128)}) custom-call(f32[2,256]{1,0:T(2,128)S(1)} %shard_map.118.part_ref, f32[2,256]{1,0:T(2,128)S(1)} %collective-permute-done.16.swapped_ref, f32[5,2,256]{2,1,0:T(2,128)S(1)} %get-tuple-element.11.ready_ref), custom_call_target="tpu_custom_call" | custom-call | tf_op jit(solution)/shard_map/pallas_call | solution.py:301
  51.1 5.0 %all-to-all-start = ((f32[32,1,128]{2,1,0:T(1,128)}), f32[32,1,128]{2,1,0:T(1,128)S(1)}, u32[]{:S(2)}, u32[]{:S(2)}) async-start(f32[32,1,128]{2,1,0:T(1,128)} %get-tuple-element.12), calls=%async_computation | async-start | bytes 32768 | tf_op jit(solution)/shard_map/all_to_all | solution.py:337
  56.7 6.6 %all-to-all-done = f32[32,1,128]{2,1,0:T(1,128)S(1)} async-done(((f32[32,1,128]{2,1,0:T(1,128)}), f32[32,1,128]{2,1,0:T(1,128)S(1)}, u32[]{:S(2)}, u32[]{:S(2)}) %all-to-all-start) | async-done | bytes 16416 | tf_op jit(solution)/shard_map/all_to_all | solution.py:337
  63.3 1.1 %shard_map.121 = f32[2,128]{1,0:T(2,128)} custom-call(f32[32,128]{1,0:T(8,128)S(1)} %bitcast.11, f32[2,256]{1,0:T(2,128)S(1)} %get-tuple-element.13.gain_ref, f32[2,128]{1,0:T(2,128)S(1)} %get-tuple-element.14.live_ref), custom_call_target="tpu_custom_call" | custom-call | tf_op jit(solution)/shard_map/pallas_call | solution.py:340
  (45 shorter events, 8.9 us)
Async XLA Ops:
  0.6 34.2 %collective-permute-start = (bf16[2,128,4096]{2,1,0:T(8,128)(2,1)}, bf16[2,128,4096]{2,1,0:T(8,128)(2,1)S(1)}, u32[]{:S(2)}, u32[]{:S(2)}) collective-permute-start(bf16[2,128,4096]{2,1,0:T(8,128)(2,1)} %param.10), channel_id=1, source_target_pairs={{0,1},{1,0},{2,3},{3,2},{4,5},{5,4},{6,7},{7,6},{8,9},{9,8},{10,11... | collective-permute-start | bytes 6291464 | tf_op jit(solution)/shard_map/ppermute | solution.py:251
  1.7 10.5 %collective-permute-start.1 = (bf16[256,512]{1,0:T(8,128)(2,1)S(1)}, bf16[256,512]{1,0:T(8,128)(2,1)S(1)}, u32[]{:S(2)}, u32[]{:S(2)}) collective-permute-start(bf16[256,512]{1,0:T(8,128)(2,1)S(1)} %constant_dynamic-slice_fusion.1.refs_0_), channel_id=1, source_target_pairs={{0,8},{1,9},{2,10},{3,11},{4,12},{5,13},{6,14},{7,15},{8,24},{9,25... | collective-permute-start | bytes 786440 | tf_op jit(solution)/shard_map/ppermute | solution.py:254
  4.8 9.0 %collective-permute-start.14 = (bf16[256,512]{1,0:T(8,128)(2,1)S(1)}, bf16[256,512]{1,0:T(8,128)(2,1)S(1)}, u32[]{:S(2)}, u32[]{:S(2)}) collective-permute-start(bf16[256,512]{1,0:T(8,128)(2,1)S(1)} %constant_dynamic-slice_fusion.1.refs_0_), channel_id=1, source_target_pairs={{0,2},{1,5},{2,0},{3,7},{4,6},{5,1},{6,4},{7,3},{8,10},{9,13},{10,... | collective-permute-start | bytes 786440 | tf_op jit(solution)/shard_map/ppermute | solution.py:254
  6.3 9.0 %collective-permute-start.13 = (bf16[256,512]{1,0:T(8,128)(2,1)S(1)}, bf16[256,512]{1,0:T(8,128)(2,1)S(1)}, u32[]{:S(2)}, u32[]{:S(2)}) collective-permute-start(bf16[256,512]{1,0:T(8,128)(2,1)S(1)} %constant_dynamic-slice_fusion.1.refs_0_), channel_id=1, source_target_pairs={{0,4},{1,3},{2,6},{3,1},{4,0},{5,7},{6,2},{7,5},{8,12},{9,11},{10,... | collective-permute-start | bytes 786440 | tf_op jit(solution)/shard_map/ppermute | solution.py:254
  7.8 9.9 %collective-permute-start.7 = (bf16[256,512]{1,0:T(8,128)(2,1)S(1)}, bf16[256,512]{1,0:T(8,128)(2,1)S(1)}, u32[]{:S(2)}, u32[]{:S(2)}) collective-permute-start(bf16[256,512]{1,0:T(8,128)(2,1)S(1)} %constant_dynamic-slice_fusion.1.refs_0_), channel_id=1, source_target_pairs={{0,16},{1,17},{2,18},{3,19},{4,20},{5,21},{6,22},{7,23},{8,0},{9,1... | collective-permute-start | bytes 786440 | tf_op jit(solution)/shard_map/ppermute | solution.py:254
  12.2 9.2 %collective-permute-start.4 = (bf16[256,512]{1,0:T(8,128)(2,1)S(1)}, bf16[256,512]{1,0:T(8,128)(2,1)S(1)}, u32[]{:S(2)}, u32[]{:S(2)}) collective-permute-start(bf16[256,512]{1,0:T(8,128)(2,1)S(1)} %collective-permute-done.1.refs_0_), channel_id=1, source_target_pairs={{0,2},{1,5},{2,0},{3,7},{4,6},{5,1},{6,4},{7,3},{8,10},{9,13},{10,... | collective-permute-start | bytes 786440 | tf_op jit(solution)/shard_map/ppermute | solution.py:254
  13.8 11.2 %collective-permute-start.15 = (bf16[256,512]{1,0:T(8,128)(2,1)S(1)}, bf16[256,512]{1,0:T(8,128)(2,1)S(1)}, u32[]{:S(2)}, u32[]{:S(2)}) collective-permute-start(bf16[256,512]{1,0:T(8,128)(2,1)S(1)} %collective-permute-done.14.refs_1_), channel_id=1, source_target_pairs={{0,4},{1,3},{2,6},{3,1},{4,0},{5,7},{6,2},{7,5},{8,12},{9,11},{10,... | collective-permute-start | bytes 786440 | tf_op jit(solution)/shard_map/ppermute | solution.py:254
  15.3 13.5 %collective-permute-start.11 = (bf16[256,512]{1,0:T(8,128)(2,1)S(1)}, bf16[256,512]{1,0:T(8,128)(2,1)S(1)}, u32[]{:S(2)}, u32[]{:S(2)}) collective-permute-start(bf16[256,512]{1,0:T(8,128)(2,1)S(1)} %collective-permute-done.1.refs_0_), channel_id=1, source_target_pairs={{0,4},{1,3},{2,6},{3,1},{4,0},{5,7},{6,2},{7,5},{8,12},{9,11},{10,... | collective-permute-start | bytes 786440 | tf_op jit(solution)/shard_map/ppermute | solution.py:254
  17.7 13.2 %collective-permute-start.9 = (bf16[256,512]{1,0:T(8,128)(2,1)S(1)}, bf16[256,512]{1,0:T(8,128)(2,1)S(1)}, u32[]{:S(2)}, u32[]{:S(2)}) collective-permute-start(bf16[256,512]{1,0:T(8,128)(2,1)S(1)} %collective-permute-done.7.refs_0_), channel_id=1, source_target_pairs={{0,2},{1,5},{2,0},{3,7},{4,6},{5,1},{6,4},{7,3},{8,10},{9,13},{10,... | collective-permute-start | bytes 786440 | tf_op jit(solution)/shard_map/ppermute | solution.py:254
  21.4 9.6 %collective-permute-start.2 = (bf16[256,512]{1,0:T(8,128)(2,1)S(1)}, bf16[256,512]{1,0:T(8,128)(2,1)S(1)}, u32[]{:S(2)}, u32[]{:S(2)}) collective-permute-start(bf16[256,512]{1,0:T(8,128)(2,1)S(1)} %collective-permute-done.1.refs_0_), channel_id=1, source_target_pairs={{0,8},{1,9},{2,10},{3,11},{4,12},{5,13},{6,14},{7,15},{8,24},{9,25... | collective-permute-start | bytes 786440 | tf_op jit(solution)/shard_map/ppermute | solution.py:254
  25.0 8.8 %collective-permute-start.5 = (bf16[256,512]{1,0:T(8,128)(2,1)S(1)}, bf16[256,512]{1,0:T(8,128)(2,1)S(1)}, u32[]{:S(2)}, u32[]{:S(2)}) collective-permute-start(bf16[256,512]{1,0:T(8,128)(2,1)S(1)} %collective-permute-done.4.refs_1_), channel_id=1, source_target_pairs={{0,8},{1,9},{2,10},{3,11},{4,12},{5,13},{6,14},{7,15},{8,24},{9,25... | collective-permute-start | bytes 786440 | tf_op jit(solution)/shard_map/ppermute | solution.py:254
  28.8 12.1 %collective-permute-start.8 = (bf16[256,512]{1,0:T(8,128)(2,1)S(1)}, bf16[256,512]{1,0:T(8,128)(2,1)S(1)}, u32[]{:S(2)}, u32[]{:S(2)}) collective-permute-start(bf16[256,512]{1,0:T(8,128)(2,1)S(1)} %collective-permute-done.7.refs_0_), channel_id=1, source_target_pairs={{0,4},{1,3},{2,6},{3,1},{4,0},{5,7},{6,2},{7,5},{8,12},{9,11},{10,... | collective-permute-start | bytes 786440 | tf_op jit(solution)/shard_map/ppermute | solution.py:254
  30.9 9.2 %collective-permute-start.12 = (bf16[256,512]{1,0:T(8,128)(2,1)S(1)}, bf16[256,512]{1,0:T(8,128)(2,1)S(1)}, u32[]{:S(2)}, u32[]{:S(2)}) collective-permute-start(bf16[256,512]{1,0:T(8,128)(2,1)S(1)} %collective-permute-done.4.refs_1_), channel_id=1, source_target_pairs={{0,4},{1,3},{2,6},{3,1},{4,0},{5,7},{6,2},{7,5},{8,12},{9,11},{10,... | collective-permute-start | bytes 786440 | tf_op jit(solution)/shard_map/ppermute | solution.py:254
  31.0 9.9 %collective-permute-start.10 = (bf16[256,512]{1,0:T(8,128)(2,1)S(1)}, bf16[256,512]{1,0:T(8,128)(2,1)S(1)}, u32[]{:S(2)}, u32[]{:S(2)}) collective-permute-start(bf16[256,512]{1,0:T(8,128)(2,1)S(1)} %collective-permute-done.9.refs_1_), channel_id=1, source_target_pairs={{0,4},{1,3},{2,6},{3,1},{4,0},{5,7},{6,2},{7,5},{8,12},{9,11},{10,... | collective-permute-start | bytes 786440 | tf_op jit(solution)/shard_map/ppermute | solution.py:254
  33.8 9.9 %collective-permute-start.3 = (bf16[256,512]{1,0:T(8,128)(2,1)S(1)}, bf16[256,512]{1,0:T(8,128)(2,1)S(1)}, u32[]{:S(2)}, u32[]{:S(2)}) collective-permute-start(bf16[256,512]{1,0:T(8,128)(2,1)S(1)} %collective-permute-done.2.refs_0_), channel_id=1, source_target_pairs={{0,4},{1,3},{2,6},{3,1},{4,0},{5,7},{6,2},{7,5},{8,12},{9,11},{10,... | collective-permute-start | bytes 786440 | tf_op jit(solution)/shard_map/ppermute | solution.py:254
  34.8 11.7 %collective-permute-start.6 = (bf16[256,512]{1,0:T(8,128)(2,1)S(1)}, bf16[256,512]{1,0:T(8,128)(2,1)S(1)}, u32[]{:S(2)}, u32[]{:S(2)}) collective-permute-start(bf16[256,512]{1,0:T(8,128)(2,1)S(1)} %collective-permute-done.5.refs_1_), channel_id=1, source_target_pairs={{0,4},{1,3},{2,6},{3,1},{4,0},{5,7},{6,2},{7,5},{8,12},{9,11},{10,... | collective-permute-start | bytes 786440 | tf_op jit(solution)/shard_map/ppermute | solution.py:254
  35.8 1.6 %copy-start.1 = (bf16[2,128,4096]{2,1,0:T(8,128)(2,1)S(1)}, bf16[2,128,4096]{2,1,0:T(8,128)(2,1)}, u32[]{:S(2)}) copy-start(bf16[2,128,4096]{2,1,0:T(8,128)(2,1)} %param.10) | copy-start | bytes 6291460
  46.5 2.5 %copy-start.6 = (s32[2]{0:T(128)S(1)}, s32[2]{0:T(128)}, u32[]{:S(2)}) copy-start(s32[2]{0:T(128)} %lengths_ref.1) | copy-start | bytes 28
  46.5 2.5 %copy-start.7 = (f32[2]{0:T(128)S(1)}, f32[2]{0:T(128)}, u32[]{:S(2)}) copy-start(f32[2]{0:T(128)} %discount_ref.1) | copy-start | bytes 28
  46.5 2.5 %copy-start.8 = (f32[2]{0:T(128)S(1)}, f32[2]{0:T(128)}, u32[]{:S(2)}) copy-start(f32[2]{0:T(128)} %trace_ref.1) | copy-start | bytes 28
  47.3 2.3 %collective-permute-start.16 = (f32[2,256]{1,0:T(2,128)S(1)}, f32[2,256]{1,0:T(2,128)S(1)}, u32[]{:S(2)}, u32[]{:S(2)}) collective-permute-start(f32[2,256]{1,0:T(2,128)S(1)} %shard_map.118.part_ref), channel_id=1, source_target_pairs={{0,1},{1,0},{2,3},{3,2},{4,5},{5,4},{6,7},{7,6},{8,9},{9,8},{10,11... | collective-permute-start | bytes 6152 | tf_op jit(solution)/shard_map/ppermute | solution.py:290
  47.4 1.3 %collective-permute-start.17 = (f32[2,128]{1,0:T(2,128)S(1)}, f32[2,128]{1,0:T(2,128)S(1)}, u32[]{:S(2)}, u32[]{:S(2)}) collective-permute-start(f32[2,128]{1,0:T(2,128)S(1)} %copy-done.4), channel_id=1, source_target_pairs={{0,1},{1,0},{2,3},{3,2},{4,5},{5,4},{6,7},{7,6},{8,9},{9,8},{10,11... | collective-permute-start | bytes 3080 | tf_op jit(solution)/shard_map/ppermute | solution.py:276
  47.9 1.2 %collective-permute-start.18 = (s32[2,128]{1,0:T(2,128)S(1)}, s32[2,128]{1,0:T(2,128)S(1)}, u32[]{:S(2)}, u32[]{:S(2)}) collective-permute-start(s32[2,128]{1,0:T(2,128)S(1)} %copy-done.5), channel_id=1, source_target_pairs={{0,1},{1,0},{2,3},{3,2},{4,5},{5,4},{6,7},{7,6},{8,9},{9,8},{10,11... | collective-permute-start | bytes 3080 | tf_op jit(solution)/shard_map/ppermute | solution.py:277
  51.1 12.2 %all-to-all-start = ((f32[32,1,128]{2,1,0:T(1,128)}), f32[32,1,128]{2,1,0:T(1,128)S(1)}, u32[]{:S(2)}, u32[]{:S(2)}) async-start(f32[32,1,128]{2,1,0:T(1,128)} %get-tuple-element.12), calls=%async_computation | async-start | bytes 32768 | tf_op jit(solution)/shard_map/all_to_all | solution.py:337
  (5 other events, 4.6 us)
